TPU v7x, 256 devices: a whole 4x4x8 slice. The times are simulated.
256 devices in a mesh: seq: 64 (over z, x, core), head: 4 (over y).
Axes of the slice: x: 4, y: 4, z: 8, core: 2. Of those that a mesh axis runs over, the one named last changes fastest.
Arguments:
- tokens: bfloat16 [65536, 2048], P('seq', 'head'), may hold values from -8 to 8
- w_query: bfloat16 [2048, 2048], P(None, 'head'), may hold values from -1 to 1, as said below
- w_key: bfloat16 [2048, 2048], P(None, 'head'), may hold values from -1 to 1, as said below
- w_value: bfloat16 [2048, 2048], P(None, 'head'), may hold values from -0.125 to 0.125
- w_out: bfloat16 [2048, 2048], P('head'), may hold values from -0.125 to 0.125
- mix_logit: float32 [8], P('head'), may hold values from -2 to 2
Outputs:
- layer_out: bfloat16 [65536, 2048], P('seq', 'head')
Inputs may be any that keep to these rules, and one draw needn't show every extreme that they name: `w_query`: entries of mean zero with a standard deviation of about 2048 ** -0.5. `w_key`: entries of mean zero with a standard deviation of about 2048 ** -0.5.
All inputs are finite; a program needn't handle non-finite values.
Results may differ from a plain program's by a relative error of at most 0.0065.
Values may be sent and summed in bfloat16 or wider, within the bound.
A program may use at most 128 MiB of HBM per device.

v0:
```python
import jax
import jax.numpy as jnp
from jax import lax
from jax.sharding import Mesh
from jax.sharding import PartitionSpec as P

SEQ = ("seq_0", "seq_1", "seq_2")


def nothing_yet(shard, identity):
    return jax.tree.map(
        lambda a, e: jnp.broadcast_to(jnp.asarray(e, a.dtype), a.shape), shard, identity
    )


def carried_in(shard, axes, combine, identity):
    before = start = nothing_yet(shard, identity)
    running = shard
    for axis in reversed(axes):
        length, mine = (lax.axis_size(axis), lax.axis_index(axis))
        pieces = jax.tree.map(
            lambda part, kind: lax.all_gather(part.astype(kind), axis),
            running,
            (jnp.bfloat16, jnp.bfloat16),
        )
        inside, running = (start, start)
        for k in range(length):
            passed = k < mine
            running = combine(
                running, jax.tree.map(lambda part, own: part[k].astype(own.dtype), pieces, shard)
            )
            inside = jax.tree.map(lambda new, old: jnp.where(passed, new, old), running, inside)
        before = combine(inside, before)
    return before


def feature(values):
    return jax.nn.elu(values) + 1.0


def add_pairs(earlier, later):
    return (earlier[0] + later[0], earlier[1] + later[1])


def on_device(tokens, w_query, w_key, w_value, w_out, mix_logit):
    seg = tokens.shape[0]
    heads = mix_logit.shape[0]
    width = w_query.shape[1]
    hsize = width // heads
    empty = jnp.zeros((seg, width), jnp.float32)
    totals = (empty, empty, empty)
    piece = lax.all_gather(tokens, "head", axis=1, tiled=True)
    result = []
    for total, weight in zip(totals, (w_query, w_key, w_value)):
        result.append(jnp.dot(piece, weight, preferred_element_type=jnp.float32))
    query, keys, values = tuple(result)
    query = query.astype(jnp.bfloat16).reshape(seg, heads, hsize)
    keys = keys.astype(jnp.bfloat16).reshape(seg, heads, hsize)
    values = values.astype(jnp.bfloat16).reshape(seg, heads, hsize)
    fkey = feature(keys.astype(jnp.float32)).astype(jnp.bfloat16)
    mem_term = jnp.einsum("thd,the->hde", fkey, values, preferred_element_type=jnp.float32)
    norm_term = jnp.sum(fkey.astype(jnp.float32), axis=0)
    zeros_pair = (jnp.zeros_like(mem_term), jnp.zeros_like(norm_term))
    memory, normal = carried_in((mem_term, norm_term), SEQ, add_pairs, zeros_pair)
    rows = lax.broadcasted_iota(jnp.int32, (seg, seg), 0)
    cols = lax.broadcasted_iota(jnp.int32, (seg, seg), 1)
    causal = cols <= rows
    scale = 1.0 / hsize**0.5
    scores = jnp.einsum("qhd,khd->hqk", query, keys, preferred_element_type=jnp.float32) * scale
    scores = jnp.where(causal[None], scores, -1e30)
    expo = jnp.exp(scores - jnp.max(scores, axis=2, keepdims=True))
    probs = (expo / jnp.sum(expo, axis=2, keepdims=True)).astype(jnp.bfloat16)
    local = jnp.einsum("hqk,khd->qhd", probs, values, preferred_element_type=jnp.float32)
    fquery = feature(query.astype(jnp.float32)).astype(jnp.bfloat16).astype(jnp.float32)
    numer = jnp.einsum("thd,hde->the", fquery, memory, precision=lax.Precision.HIGHEST)
    denom = jnp.einsum("thd,hd->th", fquery, normal, precision=lax.Precision.HIGHEST)
    readout = numer / jnp.maximum(denom, 1.0)[:, :, None]
    share = jax.nn.sigmoid(mix_logit)[None, :, None]
    mixed = (share * readout + (1.0 - share) * local).astype(jnp.bfloat16).reshape(seg, width)
    columns = lax.all_to_all(w_out, "head", split_axis=1, concat_axis=0, tiled=True)
    summed = jnp.dot(
        lax.all_gather(mixed, "head", axis=1, tiled=True),
        columns,
        preferred_element_type=jnp.float32,
    )
    return summed.astype(jnp.bfloat16)


def solution(mesh):
    torus = Mesh(
        mesh.devices.reshape(8, 4, 2, mesh.shape["head"]), ("seq_0", "seq_1", "seq_2", "head")
    )
    return jax.shard_map(
        on_device,
        mesh=torus,
        in_specs=(
            P(SEQ, "head"),
            P(None, "head"),
            P(None, "head"),
            P(None, "head"),
            P("head", None),
            P("head"),
        ),
        out_specs=P(SEQ, "head"),
        check_vma=False,
    )
```

profile of v0, /device:TPU:1, one launch (start us, length us, event | category | flops | bytes accessed | tf_op | source)
XLA Modules:
  0.0 251.1 jit_solution(9462103053753191697)
XLA Ops:
  6.5 0.0 copy-start
  6.5 0.0 all-gather.6.cloned.1.call-start
  6.5 0.7 all-gather.6.cloned.1.call-update
  7.3 0.0 all-gather.8.cloned.1.call-start
  7.3 56.3 %all-gather.6.cloned.1.call-done = bf16[1024,2048]{1,0:T(8,128)(2,1)} async-done(((bf16[1024,512]{1,0:T(8,128)(2,1)}), bf16[1024,2048]{1,0:T(8,128)(2,1)}) %all-gather.6.cloned.1.call-update) | async-done | bytes 4194320 | tf_op jit(solution)/shard_map/all_gather | solution.py:52
  63.6 0.0 copy-done
  63.6 6.2 %fusion.20 = (bf16[512]{0:T(512)(128)(2,1)S(1)}, bf16[1024,512]{0,1:T(8,128)(2,1)}) fusion(bf16[1024,2048]{1,0:T(8,128)(2,1)} %all-gather.6.cloned.1.call-done, bf16[2048,512]{1,0:T(8,128)(2,1)S(1)} %copy-done), kind=kOutput, calls=%fused_computation.36 | convolution fusion | flops 2151677440 | bytes 7341056 | tf_op jit(solution)/shard_map/dot_general | solution.py:55
  69.8 2.3 copy.33
  72.1 0.0 copy-start.1
  72.1 5.3 %convolution_convert_fusion.2 = bf16[1024,512]{0,1:T(8,128)(2,1)S(1)} fusion(bf16[1024,2048]{1,0:T(8,128)(2,1)} %all-gather.6.cloned.1.call-done, bf16[2048,512]{1,0:T(8,128)(2,1)} %param.9), kind=kOutput, calls=%fused_computation.31 | convolution fusion | flops 2148007936 | bytes 7340032 | tf_op jit(solution)/shard_map/dot_general | solution.py:55
  77.4 0.0 copy-start.3
  77.4 0.0 copy-done.1
  77.4 0.0 copy-start.2
  77.4 1.2 convolution_convert_fusion.4
  78.7 0.0 copy-done.3
  78.7 2.7 %all-gather = bf16[4,256,256]{2,1,0:T(8,128)(2,1)S(1)} all-gather(bf16[2,256,256]{2,1,0:T(8,128)(2,1)S(1)} %convolution_convert_fusion.4), channel_id=2, replica_groups=mesh['seq_0'=8,'seq_1'=4,'seq_2'=2,'head'=4] {'seq_2'}, dimensions={0}, use_global_device_ids=true | all-gather | bytes 786432 | tf_op jit(solution)/shard_map/all_gather | solution.py:22
  81.3 0.8 fusion.59
  82.1 0.0 all-gather.8.cloned.1.call-update
  82.1 0.0 all-gather.10.cloned.1.call-start
  82.2 0.0 copy-done.2
  82.2 24.7 %all-gather.8.cloned.1.call-done = bf16[4,2,256,256]{3,2,1,0:T(8,128)(2,1)} async-done(((bf16[1,2,256,256]{3,2,1,0:T(8,128)(2,1)}), bf16[4,2,256,256]{3,2,1,0:T(8,128)(2,1)}) %all-gather.8.cloned.1.call-update) | async-done | bytes 1048592 | tf_op jit(solution)/shard_map/all_gather | solution.py:22
  106.9 2.0 fusion.55
  108.9 0.0 all-gather.10.cloned.1.call-update
  108.9 0.0 all-gather.12.cloned.1.call-start
  109.0 1.3 iota_compare_fusion
  110.3 6.2 %convolution_convert_fusion.1 = bf16[1024,512]{0,1:T(8,128)(2,1)} fusion(bf16[1024,2048]{1,0:T(8,128)(2,1)} %all-gather.6.cloned.1.call-done, bf16[2048,512]{1,0:T(8,128)(2,1)} %param.7), kind=kOutput, calls=%fused_computation.30 | convolution fusion | flops 2148007936 | bytes 7340032 | tf_op jit(solution)/shard_map/dot_general | solution.py:55
  116.5 2.3 copy.36
  118.8 4.2 %all_gather.40 = bf16[2,2,256]{2,1,0:T(2,128)(2,1)S(1)} all-gather(bf16[1,2,256]{2,1,0:T(2,128)(2,1)S(1)} %all_gather.39), channel_id=1, replica_groups=mesh['seq_0'=8,'seq_1'=4,'seq_2'=2,'head'=4] {'seq_2'}, dimensions={0}, use_global_device_ids=true | all-gather | bytes 3072 | tf_op jit(solution)/shard_map/all_gather | solution.py:22
  123.0 6.7 %all_gather.41 = bf16[4,2,256]{2,1,0:T(2,128)(2,1)S(1)} all-gather(bf16[1,2,256]{2,1,0:T(2,128)(2,1)S(1)} %fusion.106), channel_id=1, replica_groups=mesh['seq_0'=8,'seq_1'=4,'seq_2'=2,'head'=4] {'seq_1'}, dimensions={0}, use_global_device_ids=true | all-gather | bytes 5120 | tf_op jit(solution)/shard_map/all_gather | solution.py:22
  129.7 14.9 %all_gather.42 = bf16[8,2,256]{2,1,0:T(2,128)(2,1)S(1)} all-gather(bf16[1,2,256]{2,1,0:T(2,128)(2,1)S(1)} %fusion.105), channel_id=1, replica_groups=mesh['seq_0'=8,'seq_1'=4,'seq_2'=2,'head'=4] {'seq_0'}, dimensions={0}, use_global_device_ids=true | all-gather | bytes 9216 | tf_op jit(solution)/shard_map/all_gather | solution.py:22
  144.6 2.8 %fusion.56 = f32[2,1,1024]{2,1,0:T(1,128)S(1)} fusion(bf16[1024,2,256]{2,0,1:T(8,128)(2,1)} %copy.36, f32[2,256,1]{1,0,2:T(2,128)S(1)} %fusion.94), kind=kOutput, calls=%fused_computation.76 | convolution fusion | flops 9437184 | bytes 1058816 | tf_op jit(solution)/shard_map/thd,hd->th/dot_general | solution.py:76
  147.4 8.4 %fusion.115 = (f32[2,1024]{1,0:T(2,128)S(1)}, f32[2,1024,1024]{1,2,0:T(8,128)}) fusion(pred[1024,1024]{0,1:T(8,128)(4,1)} %iota_compare_fusion, bf16[1024,2,256]{0,2,1:T(8,128)(2,1)} %bitcast.57, bf16[1024,2,256]{0,2,1:T(8,128)(2,1)} %bitcast.54), kind=kOutput, calls=%fused_computation.145 | convolution fusion | flops 1082131456 | bytes 11542528 | tf_op jit(solution)/shard_map/sub | solution.py:71
  155.8 6.3 %fusion.4 = f32[2,256,1024]{2,1,0:T(8,128)} fusion(bf16[1024,2,256]{0,2,1:T(8,128)(2,1)} %bitcast.59, f32[2,1024,1024]{1,2,0:T(8,128)} %get-tuple-element.8, f32[2,1024]{1,0:T(2,128)S(1)} %get-tuple-element.7), kind=kOutput, calls=%fused_computation.14 | convolution fusion | flops 1077936128 | bytes 11542528 | tf_op jit(solution)/shard_map/hqk,khd->qhd/dot_general | solution.py:73
  162.1 0.0 all-gather.10.cloned.1.call-done
  162.1 7.4 %fusion.15 = bf16[1024,2,256]{0,2,1:T(8,128)(2,1)} fusion(f32[2,256,1024]{2,1,0:T(8,128)} %fusion.4, f32[2]{0:T(128)S(1)} %get-tuple-element.5, f32[1024,2]{0,1:T(2,128)S(1)} %fusion.90, f32[2]{0:T(128)S(1)} %get-tuple-element.6, bf16[1024,2,256]{2,0,1:T(8,128)(2,1)} %copy.36, bf16[8,2,256,256]{3,2,1,0:T(8,128)(2,1)} %all-gather.10.cloned.1.call-done, ...), kind=kOutput, calls=%fused_computation.26 | convolution fusion | flops 1621753856 | bytes 7872542 | tf_op jit(solution)/shard_map/thd,hde->the/dot_general | solution.py:75
  169.5 0.0 all-gather.12.cloned.1.call-update
  169.5 4.0 %copy.41 = bf16[512,2048]{0,1:T(8,128)(2,1)} copy(bf16[512,2048]{1,0:T(8,128)(2,1)} %param.10) | data formatting | bytes 4194304 | tf_op args[4]
  173.5 39.7 %all_to_all.19 = bf16[512,4,512]{0,2,1:T(8,128)(2,1)} all-to-all(bf16[512,4,512]{0,2,1:T(8,128)(2,1)} %bitcast.51), channel_id=1, replica_groups=mesh['seq_0'=8,'seq_1'=4,'seq_2'=2,'head'=4] {'head'}, dimensions={1} | all-to-all | bytes 4194304 | tf_op jit(solution)/shard_map/all_to_all | solution.py:80
  213.2 4.2 %copy.42 = bf16[4,512,512]{2,1,0:T(8,128)(2,1)} copy(bf16[4,512,512]{1,2,0:T(8,128)(2,1)} %bitcast.50) | data formatting | bytes 4194304 | tf_op jit(solution)/shard_map/all_to_all | solution.py:80
  217.4 21.0 %all-gather.12.cloned.1.call-done = bf16[1024,2048]{0,1:T(8,128)(2,1)} async-done(((bf16[1024,512]{0,1:T(8,128)(2,1)}), bf16[1024,2048]{0,1:T(8,128)(2,1)}) %all-gather.12.cloned.1.call-update) | async-done | bytes 4194320 | tf_op jit(solution)/shard_map/all_gather | solution.py:82
  238.4 6.2 %convolution_convert_fusion = bf16[1024,512]{1,0:T(8,128)(2,1)} fusion(bf16[1024,2048]{0,1:T(8,128)(2,1)} %all-gather.12.cloned.1.call-done, bf16[2048,512]{1,0:T(8,128)(2,1)} %bitcast.52), kind=kOutput, calls=%fused_computation.29 | convolution fusion | flops 2148007936 | bytes 7340032 | tf_op jit(solution)/shard_map/dot_general | solution.py:81
  (6 shorter events, 0.1 us)
Async XLA Ops:
  6.5 57.0 %copy-start = (bf16[2048,512]{1,0:T(8,128)(2,1)S(1)}, bf16[2048,512]{1,0:T(8,128)(2,1)}, u32[]{:S(2)}) copy-start(bf16[2048,512]{1,0:T(8,128)(2,1)} %param.8) | copy-start | bytes 6291460
  6.5 57.0 %all-gather.6.cloned.1.call-start = ((), (), s32[]{:S(2)}) async-start(), calls=%async_computation.1 | async-start | bytes 5242880 | tf_op jit(solution)/shard_map/all_gather | solution.py:52
  7.3 99.6 %all-gather.8.cloned.1.call-start = ((), (), s32[]{:S(2)}) async-start(), calls=%async_computation.2 | async-start | bytes 1310720 | tf_op jit(solution)/shard_map/all_gather | solution.py:22
  72.1 5.3 %copy-start.1 = (bf16[1024,2,256]{2,0,1:T(8,128)(2,1)S(1)}, bf16[1024,2,256]{2,0,1:T(8,128)(2,1)}, u32[]{:S(2)}) copy-start(bf16[1024,2,256]{2,0,1:T(8,128)(2,1)} %copy.33) | copy-start | bytes 3145732
  77.4 1.3 copy-start.3
  77.4 4.8 %copy-start.2 = (f32[2]{0:T(128)S(1)}, f32[2]{0:T(128)}, u32[]{:S(2)}) copy-start(f32[2]{0:T(128)} %param.11) | copy-start | bytes 28
  82.1 80.0 %all-gather.10.cloned.1.call-start = ((), (), s32[]{:S(2)}) async-start(), calls=%async_computation.3 | async-start | bytes 2359296 | tf_op jit(solution)/shard_map/all_gather | solution.py:22
  108.9 129.4 %all-gather.12.cloned.1.call-start = ((), (), s32[]{:S(2)}) async-start(), calls=%async_computation.4 | async-start | bytes 5242880 | tf_op jit(solution)/shard_map/all_gather | solution.py:82
Sparse Core Ops, SparseCore 0:
  9.1 54.3 all-gather.5
  82.2 24.5 all-gather.7
  109.0 39.1 all-gather.9
  169.6 68.6 all-gather.11
where the time goes:
time: 252 us; the launch traced here: 251 us
  waiting for transfers between devices  103 us (41%)
  blocking collectives  68.1 us (27%)
  matrix products  50.1 us (20%)
  between operations  13.2 us (5%)
  local copies, waits for them, and re-layouts  12.8 us (5%)
  other arithmetic  4.18 us (2%)
    all_gather x1, waiting for transfers between devices, on_device(): piece = lax.all_gather(tokens, 'head', axis=1, tiled=True)  56.3 us
    all_to_all x1, blocking collectives, on_device(): lax.all_to_all(w_out, 'head', split_axis=1, concat_axis=0, tiled=True)  39.7 us
    all_gather x4, blocking collectives, carried_in(): lax.all_gather(part.astype(kind), axis)  28.4 us
    all_gather x2, waiting for transfers between devices, carried_in(): lax.all_gather(part.astype(kind), axis)  24.7 us
    all_gather x1, waiting for transfers between devices, on_device(): lax.all_gather(mixed, 'head', axis=1, tiled=True)  21 us
    dot_general x3, matrix products, on_device(): result.append(jnp.dot(piece, weight, preferred_element_type=jnp.float32))  17.7 us
    sub x1, matrix products, on_device(): expo = jnp.exp(scores - jnp.max(scores, axis=2, keepdims=True))  8.38 us
    dot_general x1, matrix products, on_device(): jnp.einsum('thd,hde->the', fquery, memory, precision=lax.Precision.HIGHEST)  7.36 us
  transfers between devices with their start and end apart: 4, of which 3 were waited for; matrix products, arithmetic and copies ran while one was open for 14% of the time, Pallas kernels for 0%

commit v1 on v0

--- a/solution.py
+++ b/solution.py
@@ -5,6 +5,11 @@
 from jax.sharding import PartitionSpec as P
 
 SEQ = ("seq_0", "seq_1", "seq_2")
+
+
+def gather_from_all(value, axis, dim):
+    copies = jnp.concatenate([value] * lax.axis_size(axis), axis=dim)
+    return lax.all_to_all(copies, axis, dim, dim, tiled=True)
 
 
 def nothing_yet(shard, identity):
@@ -78,11 +83,7 @@
     share = jax.nn.sigmoid(mix_logit)[None, :, None]
     mixed = (share * readout + (1.0 - share) * local).astype(jnp.bfloat16).reshape(seg, width)
     columns = lax.all_to_all(w_out, "head", split_axis=1, concat_axis=0, tiled=True)
-    summed = jnp.dot(
-        lax.all_gather(mixed, "head", axis=1, tiled=True),
-        columns,
-        preferred_element_type=jnp.float32,
-    )
+    summed = jnp.dot(gather_from_all(mixed, "head", 1), columns, preferred_element_type=jnp.float32)
     return summed.astype(jnp.bfloat16)
 
 

time: 252 us -> 232 us (0.921)
  waiting for transfers between devices: 103 us -> 69.3 us
  blocking collectives: 68.1 us -> 76.3 us
  starting transfers between devices: 0.13 us -> 4.68 us
    all_gather x1 -> x0, waiting for transfers between devices: 21 us -> none  [on_device(): lax.all_gather(mixed, 'head', axis=1, tiled=True)]
    all_gather x2, waiting for transfers between devices: 24.7 us -> 12.2 us  [carried_in(): lax.all_gather(part.astype(kind), axis)]
    all_to_all x1, blocking collectives: 39.7 us -> 48.1 us  [gather_from_all(): return lax.all_to_all(copies, axis, dim, dim, tiled=True)]
    all_to_all x0 -> x1, starting transfers between devices: none -> 4.6 us  [on_device(): lax.all_to_all(w_out, 'head', split_axis=1, concat_axis=0, tiled=True)]
  transfers between devices with their start and end apart: 4 -> 4, of which waited for: 3 -> 2; matrix products, arithmetic and copies ran while one was open for 14% -> 20% of each run, Pallas kernels for 0% -> 0%
where the time goes in v1:
time: 232 us; the launch traced here: 229 us
  blocking collectives  76.3 us (33%)
  waiting for transfers between devices  69.3 us (30%)
  matrix products  47.8 us (21%)
  local copies, waits for them, and re-layouts  13.5 us (6%)
  between operations  13.2 us (6%)
  starting transfers between devices  4.68 us (2%)
  other arithmetic  4.14 us (2%)
    all_gather x1, waiting for transfers between devices, on_device(): piece = lax.all_gather(tokens, 'head', axis=1, tiled=True)  56.3 us
    all_to_all x1, blocking collectives, gather_from_all(): return lax.all_to_all(copies, axis, dim, dim, tiled=True)  48.1 us
    all_gather x4, blocking collectives, carried_in(): lax.all_gather(part.astype(kind), axis)  28.1 us
    dot_general x3, matrix products, on_device(): result.append(jnp.dot(piece, weight, preferred_element_type=jnp.float32))  16.9 us
    all_gather x2, waiting for transfers between devices, carried_in(): lax.all_gather(part.astype(kind), axis)  12.2 us
    sub x1, matrix products, on_device(): expo = jnp.exp(scores - jnp.max(scores, axis=2, keepdims=True))  8.37 us
    dot_general x1, matrix products, on_device(): jnp.einsum('thd,hde->the', fquery, memory, precision=lax.Precision.HIGHEST)  7.37 us
    dot_general x1, matrix products, on_device(): jnp.einsum('hqk,khd->qhd', probs, values, preferred_element_type=jnp.floa...  6.28 us
  transfers between devices with their start and end apart: 4, of which 2 were waited for; matrix products, arithmetic and copies ran while one was open for 20% of the time, Pallas kernels for 0%

profile of v1, /device:TPU:1, one launch (start us, length us, event | category | flops | bytes accessed | tf_op | source)
XLA Modules:
  0.0 229.0 jit_solution(29620586906321145)
XLA Ops:
  6.5 0.0 copy-start
  6.5 0.0 all-gather.5.cloned.1.call-start
  6.5 0.7 all-gather.5.cloned.1.call-update
  7.3 0.0 all-gather.7.cloned.1.call-start
  7.3 56.3 %all-gather.5.cloned.1.call-done = bf16[1024,2048]{1,0:T(8,128)(2,1)} async-done(((bf16[1024,512]{1,0:T(8,128)(2,1)}), bf16[1024,2048]{1,0:T(8,128)(2,1)}) %all-gather.5.cloned.1.call-update) | async-done | bytes 4194320 | tf_op jit(solution)/shard_map/all_gather | solution.py:57
  63.6 0.0 copy-done
  63.6 5.3 %fusion.24 = (bf16[512]{0:T(512)(128)(2,1)S(1)}, bf16[1024,512]{0,1:T(8,128)(2,1)S(1)}) fusion(bf16[1024,2048]{1,0:T(8,128)(2,1)} %all-gather.5.cloned.1.call-done, bf16[2048,512]{1,0:T(8,128)(2,1)S(1)} %copy-done), kind=kOutput, calls=%fused_computation.38 | convolution fusion | flops 2151677440 | bytes 7341056 | tf_op jit(solution)/shard_map/dot_general | solution.py:60
  68.9 0.0 copy-start.1
  68.9 1.3 copy.27
  70.2 0.0 copy-start.2
  70.2 5.3 %convolution_convert_fusion.1 = bf16[1024,512]{0,1:T(8,128)(2,1)S(1)} fusion(bf16[1024,2048]{1,0:T(8,128)(2,1)} %all-gather.5.cloned.1.call-done, bf16[2048,512]{1,0:T(8,128)(2,1)} %param.9), kind=kOutput, calls=%fused_computation.33 | convolution fusion | flops 2148007936 | bytes 7340032 | tf_op jit(solution)/shard_map/dot_general | solution.py:60
  75.5 0.0 copy-done.1
  75.5 0.0 copy-start.4
  75.6 0.0 copy-done.2
  75.6 1.2 convolution_convert_fusion.3
  76.8 0.0 copy-done.4
  76.8 2.6 %all-gather = bf16[4,256,256]{2,1,0:T(8,128)(2,1)S(1)} all-gather(bf16[2,256,256]{2,1,0:T(8,128)(2,1)S(1)} %convolution_convert_fusion.3), channel_id=2, replica_groups=mesh['seq_0'=8,'seq_1'=4,'seq_2'=2,'head'=4] {'seq_2'}, dimensions={0}, use_global_device_ids=true | all-gather | bytes 786432 | tf_op jit(solution)/shard_map/all_gather | solution.py:27
  79.5 0.8 fusion.63
  80.3 0.0 all-gather.7.cloned.1.call-update
  80.3 3.9 %copy.36 = bf16[512,2048]{0,1:T(8,128)(2,1)} copy(bf16[512,2048]{1,0:T(8,128)(2,1)} %param.10) | data formatting | bytes 4194304 | tf_op args[4]
  84.2 4.2 %copy.37 = bf16[512,4,512]{2,0,1:T(8,128)(2,1)} copy(bf16[512,4,512]{0,2,1:T(8,128)(2,1)} %bitcast.54) | data formatting | bytes 4194304 | tf_op jit(solution)/shard_map/all_to_all | solution.py:85
  88.4 0.0 copy-start.3
  88.4 4.6 %all-to-all-start.1 = ((bf16[512,4,512]{2,0,1:T(8,128)(2,1)}), bf16[512,4,512]{2,0,1:T(8,128)(2,1)}, u32[]{:S(2)}, u32[]{:S(2)}) async-start(bf16[512,4,512]{2,0,1:T(8,128)(2,1)} %copy.37), calls=%async_computation.1 | async-start | bytes 4194304 | tf_op jit(solution)/shard_map/all_to_all | solution.py:85
  93.0 0.0 all-gather.9.cloned.1.call-start
  93.1 0.0 copy-done.3
  93.1 12.2 %all-gather.7.cloned.1.call-done = bf16[4,2,256,256]{3,2,1,0:T(8,128)(2,1)} async-done(((bf16[1,2,256,256]{3,2,1,0:T(8,128)(2,1)}), bf16[4,2,256,256]{3,2,1,0:T(8,128)(2,1)}) %all-gather.7.cloned.1.call-update) | async-done | bytes 1048592 | tf_op jit(solution)/shard_map/all_gather | solution.py:27
  105.3 2.0 fusion.59
  107.3 0.0 all-gather.9.cloned.1.call-update
  107.4 1.3 iota_compare_fusion
  108.6 6.2 %convolution_convert_fusion = bf16[1024,512]{0,1:T(8,128)(2,1)} fusion(bf16[1024,2048]{1,0:T(8,128)(2,1)} %all-gather.5.cloned.1.call-done, bf16[2048,512]{1,0:T(8,128)(2,1)} %param.7), kind=kOutput, calls=%fused_computation.32 | convolution fusion | flops 2148007936 | bytes 7340032 | tf_op jit(solution)/shard_map/dot_general | solution.py:60
  114.9 2.3 copy.30
  117.2 3.9 %all_gather.37 = bf16[2,2,256]{2,1,0:T(2,128)(2,1)S(1)} all-gather(bf16[1,2,256]{2,1,0:T(2,128)(2,1)S(1)} %all_gather.36), channel_id=1, replica_groups=mesh['seq_0'=8,'seq_1'=4,'seq_2'=2,'head'=4] {'seq_2'}, dimensions={0}, use_global_device_ids=true | all-gather | bytes 3072 | tf_op jit(solution)/shard_map/all_gather | solution.py:27
  121.1 6.5 %all_gather.38 = bf16[4,2,256]{2,1,0:T(2,128)(2,1)S(1)} all-gather(bf16[1,2,256]{2,1,0:T(2,128)(2,1)S(1)} %fusion.110), channel_id=1, replica_groups=mesh['seq_0'=8,'seq_1'=4,'seq_2'=2,'head'=4] {'seq_1'}, dimensions={0}, use_global_device_ids=true | all-gather | bytes 5120 | tf_op jit(solution)/shard_map/all_gather | solution.py:27
  127.6 15.1 %all_gather.39 = bf16[8,2,256]{2,1,0:T(2,128)(2,1)S(1)} all-gather(bf16[1,2,256]{2,1,0:T(2,128)(2,1)S(1)} %fusion.109), channel_id=1, replica_groups=mesh['seq_0'=8,'seq_1'=4,'seq_2'=2,'head'=4] {'seq_0'}, dimensions={0}, use_global_device_ids=true | all-gather | bytes 9216 | tf_op jit(solution)/shard_map/all_gather | solution.py:27
  142.7 2.8 %fusion.60 = f32[2,1,1024]{2,1,0:T(1,128)S(1)} fusion(bf16[1024,2,256]{2,0,1:T(8,128)(2,1)} %copy.30, f32[2,256,1]{1,0,2:T(2,128)S(1)} %fusion.98), kind=kOutput, calls=%fused_computation.78 | convolution fusion | flops 9437184 | bytes 1058816 | tf_op jit(solution)/shard_map/thd,hd->th/dot_general | solution.py:81
  145.5 8.4 %fusion.119 = (f32[2,1024]{1,0:T(2,128)S(1)}, f32[2,1024,1024]{1,2,0:T(8,128)}) fusion(pred[1024,1024]{0,1:T(8,128)(4,1)} %iota_compare_fusion, bf16[1024,2,256]{0,2,1:T(8,128)(2,1)} %bitcast.58, bf16[1024,2,256]{0,2,1:T(8,128)(2,1)} %bitcast.56), kind=kOutput, calls=%fused_computation.147 | convolution fusion | flops 1082131456 | bytes 11542528 | tf_op jit(solution)/shard_map/sub | solution.py:76
  153.9 6.3 %fusion.4 = f32[2,256,1024]{2,1,0:T(8,128)} fusion(bf16[1024,2,256]{0,2,1:T(8,128)(2,1)} %bitcast.61, f32[2,1024,1024]{1,2,0:T(8,128)} %get-tuple-element.8, f32[2,1024]{1,0:T(2,128)S(1)} %get-tuple-element.7), kind=kOutput, calls=%fused_computation.14 | convolution fusion | flops 1077936128 | bytes 11542528 | tf_op jit(solution)/shard_map/hqk,khd->qhd/dot_general | solution.py:78
  160.2 0.0 all-gather.9.cloned.1.call-done
  160.2 7.4 %fusion.17 = bf16[1024,2,256]{0,2,1:T(8,128)(2,1)} fusion(f32[2,256,1024]{2,1,0:T(8,128)} %fusion.4, f32[2]{0:T(128)S(1)} %get-tuple-element.5, f32[1024,2]{0,1:T(2,128)S(1)} %fusion.94, f32[2]{0:T(128)S(1)} %get-tuple-element.6, bf16[1024,2,256]{2,0,1:T(8,128)(2,1)} %copy.30, bf16[8,2,256,256]{3,2,1,0:T(8,128)(2,1)} %all-gather.9.cloned.1.call-done, ...), kind=kOutput, calls=%fused_computation.29 | convolution fusion | flops 1621753856 | bytes 7872542 | tf_op jit(solution)/shard_map/thd,hde->the/dot_general | solution.py:80
  167.6 1.5 copy.35
  169.1 0.0 all-to-all-done.1
  169.1 0.3 concatenate.7
  169.4 48.1 %all_to_all.22 = bf16[1024,4,512]{2,0,1:T(8,128)(2,1)S(1)} all-to-all(bf16[1024,4,512]{2,0,1:T(8,128)(2,1)S(1)} %concatenate.7), channel_id=1, replica_groups=mesh['seq_0'=8,'seq_1'=4,'seq_2'=2,'head'=4] {'head'}, dimensions={1} | all-to-all | bytes 8388608 | tf_op jit(solution)/shard_map/all_to_all | solution.py:12
  217.5 4.9 %bitcast_convert_fusion = bf16[1024,512]{1,0:T(8,128)(2,1)} fusion(bf16[1024,4,512]{2,0,1:T(8,128)(2,1)S(1)} %all_to_all.22, bf16[512,4,512]{2,0,1:T(8,128)(2,1)} %all-to-all-done.1), kind=kOutput, calls=%fused_computation.25 | convolution fusion | flops 2148007936 | bytes 7340032 | tf_op jit(solution)/shard_map/dot_general | solution.py:86
  (6 shorter events, 0.1 us)
Async XLA Ops:
  6.5 57.0 %copy-start = (bf16[2048,512]{1,0:T(8,128)(2,1)S(1)}, bf16[2048,512]{1,0:T(8,128)(2,1)}, u32[]{:S(2)}) copy-start(bf16[2048,512]{1,0:T(8,128)(2,1)} %param.8) | copy-start | bytes 6291460
  6.5 57.0 %all-gather.5.cloned.1.call-start = ((), (), s32[]{:S(2)}) async-start(), calls=%async_computation.2 | async-start | bytes 5242880 | tf_op jit(solution)/shard_map/all_gather | solution.py:57
  7.3 98.1 %all-gather.7.cloned.1.call-start = ((), (), s32[]{:S(2)}) async-start(), calls=%async_computation.3 | async-start | bytes 1310720 | tf_op jit(solution)/shard_map/all_gather | solution.py:27
  68.9 6.6 %copy-start.1 = (bf16[1024,512]{0,1:T(8,128)(2,1)}, bf16[1024,512]{0,1:T(8,128)(2,1)S(1)}, u32[]{:S(2)}) copy-start(bf16[1024,512]{0,1:T(8,128)(2,1)S(1)} %get-tuple-element.10) | copy-start | bytes 3145732
  70.2 5.3 %copy-start.2 = (bf16[1024,2,256]{2,0,1:T(8,128)(2,1)S(1)}, bf16[1024,2,256]{2,0,1:T(8,128)(2,1)}, u32[]{:S(2)}) copy-start(bf16[1024,2,256]{2,0,1:T(8,128)(2,1)} %copy.27) | copy-start | bytes 3145732
  75.5 1.3 copy-start.4
  88.4 4.7 %copy-start.3 = (f32[2]{0:T(128)S(1)}, f32[2]{0:T(128)}, u32[]{:S(2)}) copy-start(f32[2]{0:T(128)} %param.11) | copy-start | bytes 28
  88.4 80.7 %all-to-all-start.1 = ((bf16[512,4,512]{2,0,1:T(8,128)(2,1)}), bf16[512,4,512]{2,0,1:T(8,128)(2,1)}, u32[]{:S(2)}, u32[]{:S(2)}) async-start(bf16[512,4,512]{2,0,1:T(8,128)(2,1)} %copy.37), calls=%async_computation.1 | async-start | bytes 4194304 | tf_op jit(solution)/shard_map/all_to_all | solution.py:85
  93.0 67.2 %all-gather.9.cloned.1.call-start = ((), (), s32[]{:S(2)}) async-start(), calls=%async_computation.4 | async-start | bytes 2359296 | tf_op jit(solution)/shard_map/all_gather | solution.py:27
Sparse Core Ops, SparseCore 0:
  9.1 54.3 all-gather.4
  80.4 24.8 all-gather.6
  107.5 38.8 all-gather.8
